TPU v7x, 256 devices: a whole 4x4x8 slice. The times are simulated.
256 devices in a mesh: pop: 64 (over x, z, core), mp: 4 (over y).
Axes of the slice: x: 4, y: 4, z: 8, core: 2. Of those that a mesh axis runs over, the one named last changes fastest.
Arguments:
- tokens: bfloat16 [256, 3584], replicated, may hold values from -60 to 60
- target: bfloat16 [256, 3584], P(None, 'mp'), may hold values from -6 to 6
- w_query: bfloat16 [3584, 3584], P('pop', 'mp'), may hold values from -0.09375 to 0.09375
- w_key: bfloat16 [3584, 512], P(None, 'mp'), may hold values from -0.09375 to 0.09375
- w_value: bfloat16 [3584, 512], P(None, 'mp'), may hold values from -0.09375 to 0.09375
- w_out: bfloat16 [3584, 3584], P('mp', 'pop'), may hold values from -0.09375 to 0.09375
- query_left_factors: bfloat16 [64, 3584, 4], P('pop'), may hold values from -0.09375 to 0.09375
- query_right_factors: bfloat16 [64, 4, 3584], P('pop', None, 'mp'), may hold values from -6 to 6
- o_left: bfloat16 [64, 3584, 4], P('pop', 'mp'), may hold values from -0.09375 to 0.09375
- o_right: bfloat16 [64, 4, 3584], P('pop'), may hold values from -6 to 6
- member_ids: int32 [64], P('pop'), may hold values from 0 to 63, each once
Outputs:
- grad_query: float32 [3584, 3584], P('pop', 'mp')
- grad_out: float32 [3584, 3584], P('mp', 'pop')
- fitness: float32 [64], P('pop')
Inputs may be any that keep to these rules, and one draw needn't show every extreme that they name: `member_ids`: every number from 0 to 63 appears once.
All inputs are finite; a program needn't handle non-finite values.
Results may differ from a plain program's by a relative error of at most 0.005.
Values may be sent and summed in bfloat16 or wider, within the bound.
No kernel may reach another device: no remote copies, remote signals or barrier semaphores. Data moves between devices by JAX's collectives and lax.ppermute only.
A program may use at most 64 MiB of HBM per device.

v0:
```python
import math
import jax
import jax.numpy as jnp
from jax import lax
from jax.sharding import Mesh
from jax.sharding import PartitionSpec as P

D = 3584
HEADS = 28
KV_HEADS = 4
HEAD_DIM = 128
RANK = 4
POP = ("pop_0", "pop_1", "pop_2")
noise_scale = 0.5
rope_base = 1000000.0
spread_floor = 0.001


def in_order(parts, dim):
    parts = jnp.moveaxis(parts, 0, dim)
    shape = parts.shape
    return parts.reshape(*shape[:dim], shape[dim] * shape[dim + 1], *shape[dim + 2 :])


def all_blocks(shard, axes, turns):
    parts = shard[None]
    for k in turns:
        parts = lax.all_gather(parts, axes[k], axis=0, tiled=True)
    held = [lax.axis_size(axes[k]) for k in reversed(turns)]
    parts = parts.reshape(*held, *shard.shape)
    turned = sorted(range(len(turns)), key=lambda place: turns[len(turns) - 1 - place])
    return parts.transpose(*turned, *range(len(turns), parts.ndim)).reshape(-1, *shard.shape)


def whole_of(shard, axes, turns, dim):
    return in_order(all_blocks(shard, axes, turns), dim)


def cut_along(shard, dim, devices):
    before, after = (shard.shape[:dim], shard.shape[dim + 1 :])
    return jnp.moveaxis(shard.reshape(*before, devices, -1, *after), dim, 0)


def summed_on_arrival(shard, axis, dim):
    devices = lax.axis_size(axis)
    parts = lax.all_to_all(cut_along(shard, dim, devices), axis, 0, 0, tiled=True)
    return jnp.sum(parts.astype(jnp.float32), axis=0)


def copy_for_each(shard, axis):
    copies = jnp.broadcast_to(shard, (lax.axis_size(axis), *shard.shape))
    return lax.all_to_all(copies, axis, split_axis=0, concat_axis=0, tiled=True)


def of_everyone(shard, axis):
    return copy_for_each(shard, axis).sum(axis=0)


def gathered_copies(shard, axis, dim):
    return in_order(copy_for_each(shard, axis), dim)


def side_by_side(arrays, axis, dim, along):
    columns = [a.reshape(*a.shape[:along], -1) for a in arrays]
    both = jnp.concatenate(columns, axis=along)
    result, at, done = (lax.all_gather(both, axis, axis=dim, tiled=True), 0, [])
    for a, column in zip(arrays, columns):
        share = result[..., at : at + column.shape[along]]
        done.append(share.reshape(*share.shape[:along], *a.shape[along:]))
        at += column.shape[along]
    return tuple(done)


def tables(count, head_size):
    position = jnp.arange(count, dtype=jnp.float32)
    index = jnp.arange(head_size // 2, dtype=jnp.float32)
    freq = jnp.exp(-math.log(rope_base) * 2.0 * index / head_size)
    angle = position[:, None] * freq[None, :]
    return (jnp.cos(angle)[:, None, :], jnp.sin(angle)[:, None, :])


def rotate(field, cosine_table, sine):
    half = field.shape[-1] // 2
    first = field[..., :half]
    second = field[..., half:]
    return jnp.concatenate(
        [first * cosine_table - second * sine, second * cosine_table + first * sine], axis=-1
    )


def per_device(
    tokens,
    target,
    w_query,
    w_key,
    w_value,
    w_out,
    query_left_factors,
    query_right_factors,
    o_left,
    o_right,
    member_ids,
):
    tok = tokens.shape[0]
    local_feats = w_query.shape[1]
    local_kv = w_key.shape[1] // HEAD_DIM
    group = HEADS // KV_HEADS
    local_heads = local_kv * group
    slots = query_left_factors.shape[0]
    scale = HEAD_DIM ** (-0.5)
    cosine_table, sine = tables(tok, HEAD_DIM)
    base = jnp.dot(tokens, whole_of(w_query, POP, (0, 1, 2), 0), preferred_element_type=jnp.float32)
    keys = rotate(
        jnp.dot(tokens, w_key, preferred_element_type=jnp.float32).reshape(tok, local_kv, HEAD_DIM),
        cosine_table,
        sine,
    ).astype(jnp.bfloat16)
    values = (
        jnp.dot(tokens, w_value, preferred_element_type=jnp.float32)
        .astype(jnp.bfloat16)
        .reshape(tok, local_kv, HEAD_DIM)
    )
    signs = (1 - 2 * (member_ids % 2)).astype(jnp.float32)
    factor = noise_scale * signs[:, None, None]
    lowrank_product = jnp.einsum(
        "td,mdr->mtr", tokens, query_left_factors, preferred_element_type=jnp.float32
    ).astype(jnp.bfloat16)
    query = base[None] + factor * jnp.einsum(
        "olj,ojv->olv", lowrank_product, query_right_factors, preferred_element_type=jnp.float32
    )
    query = rotate(
        query.reshape(slots, tok, local_heads, HEAD_DIM), cosine_table[None], sine[None]
    ).astype(jnp.bfloat16)
    query = query.reshape(slots, tok, local_kv, group, HEAD_DIM)
    scores = jnp.einsum("mtkgd,skd->mkgts", query, keys, preferred_element_type=jnp.float32) * scale
    causal = jnp.arange(tok)[:, None] >= jnp.arange(tok)[None, :]
    scores = jnp.where(causal, scores, -1e30)
    probs = jax.nn.softmax(scores, axis=-1).astype(jnp.bfloat16)
    mixed = (
        jnp.einsum("mkgts,skd->mtkgd", probs, values, preferred_element_type=jnp.float32)
        .astype(jnp.bfloat16)
        .reshape(slots, tok, local_feats)
    )
    low_out = jnp.einsum("mtf,mfr->mtr", mixed, o_left, preferred_element_type=jnp.float32)
    right_full = o_right.astype(jnp.float32)
    part = jnp.einsum(
        "mtf,fe->mte",
        mixed,
        lax.all_gather(w_out, POP, axis=1, tiled=True),
        preferred_element_type=jnp.float32,
    )
    term = part + factor * jnp.einsum(
        "mtr,mre->mte", low_out, right_full, precision=lax.Precision.HIGHEST
    )
    output = summed_on_arrival(term.astype(jnp.bfloat16), "mp", 2)
    diff = output - target.astype(jnp.float32)[None]
    errors = of_everyone(jnp.sum(diff * diff, axis=(1, 2)), "mp")
    fitness = -(errors / (tok * D))
    count = slots * lax.axis_size(POP)
    everyone = gathered_copies(fitness, POP, 0)
    mean = jnp.sum(everyone) / count
    spread = jnp.sum((everyone - mean) * (everyone - mean)) / count
    weight = signs * (fitness - mean) / jnp.sqrt(spread + spread_floor)
    every_weight = gathered_copies(weight, POP, 0)
    right_factors_gathered, left_all = side_by_side((query_right_factors, o_left), POP, 0, 1)
    rows_q = lax.all_to_all(query_left_factors, POP, split_axis=1, concat_axis=0, tiled=True)
    cols_o = lax.all_to_all(o_right, POP, split_axis=2, concat_axis=0, tiled=True)
    whole_population = rows_q.shape[0]
    left_q = jnp.transpose(
        rows_q.astype(jnp.float32) * every_weight[:, None, None], (1, 0, 2)
    ).reshape(rows_q.shape[1], whole_population * RANK)
    right_q = right_factors_gathered.astype(jnp.float32).reshape(
        whole_population * RANK, local_feats
    )
    grad_query = jnp.dot(left_q, right_q, precision=lax.Precision.HIGHEST) / noise_scale
    output_left_factor = jnp.transpose(
        left_all.astype(jnp.float32) * every_weight[:, None, None], (1, 0, 2)
    ).reshape(local_feats, whole_population * RANK)
    right_o = cols_o.astype(jnp.float32).reshape(whole_population * RANK, cols_o.shape[2])
    grad_out = jnp.dot(output_left_factor, right_o, precision=lax.Precision.HIGHEST) / noise_scale
    return (grad_query, grad_out, fitness)


def solution(mesh):
    torus = Mesh(mesh.devices.reshape(4, 8, 2, mesh.shape["mp"]), ("pop_0", "pop_1", "pop_2", "mp"))
    placed = (
        P(),
        P(None, "mp"),
        P(POP, "mp"),
        P(None, "mp"),
        P(None, "mp"),
        P("mp", POP),
        P(POP, None, None),
        P(POP, None, "mp"),
        P(POP, "mp", None),
        P(POP, None, None),
        P(POP),
    )
    return jax.shard_map(
        per_device,
        mesh=torus,
        in_specs=placed,
        out_specs=(P(POP, "mp"), P("mp", POP), P(POP)),
        check_vma=False,
    )
```

profile of v0, /device:TPU:1, one launch (start us, length us, event | category | flops | bytes accessed | tf_op | source)
XLA Modules:
  0.0 428.7 jit_solution(7784847421207332163)
XLA Ops:
  7.2 13.0 %all-gather = bf16[224,896]{1,0:T(8,128)(2,1)} all-gather(bf16[56,896]{1,0:T(8,128)(2,1)} %param.13), channel_id=2, replica_groups=mesh['pop_0'=4,'pop_1'=8,'pop_2'=2,'mp'=4] {'pop_0'}, dimensions={0}, use_global_device_ids=true | all-gather | bytes 501760 | tf_op jit(solution)/shard_map/all_gather | solution.py:28
  20.3 49.6 %all-gather.6.cloned.1.call-done = bf16[32,56,896]{2,1,0:T(8,128)(2,1)} async-done(((bf16[4,56,896]{2,1,0:T(8,128)(2,1)}), bf16[32,56,896]{2,1,0:T(8,128)(2,1)}) %all-gather.6.cloned.1.call-update) | async-done | bytes 3211280 | tf_op jit(solution)/shard_map/all_gather | solution.py:28
  73.6 19.9 %all-gather.8.cloned.1.call-done = bf16[64,56,896]{2,1,0:T(8,128)(2,1)} async-done(((bf16[32,56,896]{2,1,0:T(8,128)(2,1)}), bf16[64,56,896]{2,1,0:T(8,128)(2,1)}) %all-gather.8.cloned.1.call-update) | async-done | bytes 6422544 | tf_op jit(solution)/shard_map/all_gather | solution.py:28
  93.5 3.3 copy.114
  96.9 2.1 fusion.29
  110.0 2.6 convolution_convert_fusion
  112.8 65.1 %all-gather.10.cloned.1.call-done = bf16[896,3584]{0,1:T(8,128)(2,1)} async-done(((bf16[896,56]{0,1:T(8,128)(2,1)}), bf16[896,3584]{0,1:T(8,128)(2,1)}) %all-gather.10.cloned.1.call-update) | async-done | bytes 6422544 | tf_op jit(solution)/shard_map/all_gather | solution.py:149
  177.9 4.9 %fusion.30 = f32[256,3584]{1,0:T(8,128)S(1)} fusion(bf16[256,896]{0,1:T(8,128)(2,1)S(1)} %bitcast.106, bf16[896,3584]{0,1:T(8,128)(2,1)} %all-gather.10.cloned.1.call-done), kind=kOutput, calls=%fused_computation.58 | convolution fusion | flops 1644167168 | bytes 10551296 | tf_op jit(solution)/shard_map/mtf,fe->mte/dot_general | solution.py:146
  182.8 3.1 fusion.1
  185.9 3.3 reshape.288
  190.7 4.0 all-to-all-start.1
  195.3 22.5 %all-to-all-done.1 = bf16[4,1,256,896]{3,2,1,0:T(8,128)(2,1)S(1)} async-done(((bf16[4,1,256,896]{3,2,1,0:T(8,128)(2,1)}), bf16[4,1,256,896]{3,2,1,0:T(8,128)(2,1)S(1)}, u32[]{:S(2)}, u32[]{:S(2)}) %all-to-all-start.1) | async-done | bytes 1835040 | tf_op jit(solution)/shard_map/all_to_all | solution.py:46
  219.6 6.5 %all_to_all.47 = f32[4,1,1]{2,1,0:T(1,128)S(1)} all-to-all(f32[4,1,1]{2,1,0:T(1,128)S(1)} %broadcast_in_dim.34), channel_id=1, replica_groups=mesh['pop_0'=4,'pop_1'=8,'pop_2'=2,'mp'=4] {'mp'}, dimensions={0} | all-to-all | bytes 32 | tf_op jit(solution)/shard_map/all_to_all | solution.py:52
  227.9 7.9 %all-to-all-start.3 = ((f32[64,1,1]{2,1,0:T(1,128)}), f32[64,1,1]{2,1,0:T(1,128)S(1)}, u32[]{:S(2)}, u32[]{:S(2)}) async-start(f32[64,1,1]{2,1,0:T(1,128)} %broadcast_in_dim.35), calls=%async_computation.3 | async-start | bytes 65536 | tf_op jit(solution)/shard_map/all_to_all | solution.py:52
  235.9 51.8 %all-gather.1 = bf16[64,1,7168]{2,1,0:T(2,128)(2,1)S(1)} all-gather(bf16[1,1,7168]{2,1,0:T(2,128)(2,1)S(1)} %maximum_bitcast_fusion.2), channel_id=1, replica_groups=mesh['pop_0'=4,'pop_1'=8,'pop_2'=2,'mp'=4] {'pop_0','pop_1','pop_2'}, dimensions={0}, use_global_device_ids=true | all-gather | bytes 931840 | tf_op jit(solution)/shard_map/all_gather | solution.py:66
  287.7 3.2 copy.129
  292.2 7.3 %all-to-all-start.5 = ((bf16[1,4,3584]{1,0,2:T(2,128)(2,1)}), bf16[1,4,3584]{1,0,2:T(2,128)(2,1)S(1)}, u32[]{:S(2)}, u32[]{:S(2)}) async-start(bf16[1,4,3584]{1,0,2:T(2,128)(2,1)} %copy.129), calls=%async_computation.5 | async-start | bytes 3670016 | tf_op jit(solution)/shard_map/all_to_all | solution.py:167
  301.5 3.2 copy.112
  306.1 38.7 %all-to-all-done.5 = bf16[1,4,3584]{1,0,2:T(2,128)(2,1)S(1)} async-done(((bf16[1,4,3584]{1,0,2:T(2,128)(2,1)}), bf16[1,4,3584]{1,0,2:T(2,128)(2,1)S(1)}, u32[]{:S(2)}, u32[]{:S(2)}) %all-to-all-start.5) | async-done | bytes 28704 | tf_op jit(solution)/shard_map/all_to_all | solution.py:167
  344.8 6.2 %all-to-all-start = ((bf16[1,3584,4]{2,0,1:T(2,128)(2,1)}), bf16[1,3584,4]{2,0,1:T(2,128)(2,1)}, u32[]{:S(2)}, u32[]{:S(2)}) async-start(bf16[1,3584,4]{2,0,1:T(2,128)(2,1)} %copy.112), calls=%async_computation | async-start | bytes 3670016 | tf_op jit(solution)/shard_map/all_to_all | solution.py:166
  352.3 44.0 %all-to-all-done = bf16[1,3584,4]{2,0,1:T(2,128)(2,1)} async-done(((bf16[1,3584,4]{2,0,1:T(2,128)(2,1)}), bf16[1,3584,4]{2,0,1:T(2,128)(2,1)}, u32[]{:S(2)}, u32[]{:S(2)}) %all-to-all-start) | async-done | bytes 28704 | tf_op jit(solution)/shard_map/all_to_all | solution.py:166
  396.9 6.0 %all-to-all-start.4 = ((f32[64,1,1]{2,1,0:T(1,128)}), f32[64,1,1]{2,1,0:T(1,128)S(1)}, u32[]{:S(2)}, u32[]{:S(2)}) async-start(f32[64,1,1]{2,1,0:T(1,128)} %broadcast_in_dim.36), calls=%async_computation.4 | async-start | bytes 65536 | tf_op jit(solution)/shard_map/all_to_all | solution.py:52
  408.1 3.7 copy.113
  414.4 2.8 copy.128
  (79 shorter events, 35.9 us)
Async XLA Ops:
  7.2 64.2 %copy-start = (bf16[256,3584]{1,0:T(8,128)(2,1)S(1)}, bf16[256,3584]{1,0:T(8,128)(2,1)}, u32[]{:S(2)}) copy-start(bf16[256,3584]{1,0:T(8,128)(2,1)} %param.11) | copy-start | bytes 5505028
  7.2 62.7 %all-gather.6.cloned.1.call-start = ((), (), s32[]{:S(2)}) async-start(), calls=%async_computation.6 | async-start | bytes 3612672 | tf_op jit(solution)/shard_map/all_gather | solution.py:28
  20.2 51.2 %copy-start.4 = (bf16[3584,128]{1,0:T(8,128)(2,1)S(1)}, bf16[3584,128]{1,0:T(8,128)(2,1)}, u32[]{:S(2)}) copy-start(bf16[3584,128]{1,0:T(8,128)(2,1)} %param.14) | copy-start | bytes 2752516
  20.3 73.3 %all-gather.8.cloned.1.call-start = ((), (), s32[]{:S(2)}) async-start(), calls=%async_computation.7 | async-start | bytes 9633792 | tf_op jit(solution)/shard_map/all_gather | solution.py:28
  69.9 107.9 %all-gather.10.cloned.1.call-start = ((), (), s32[]{:S(2)}) async-start(), calls=%async_computation.8 | async-start | bytes 6522880 | tf_op jit(solution)/shard_map/all_gather | solution.py:149
  96.9 2.2 copy-start.9
  96.9 2.2 copy-start.11
  106.1 1.4 copy-start.6
  106.1 1.4 copy-start.7
  108.1 1.3 copy-start.2
  108.2 1.9 copy-start.13
  110.0 2.6 copy-start.12
  112.8 70.0 %copy-start.8 = (bf16[1,4,3584]{2,1,0:T(4,128)(2,1)S(1)}, bf16[1,4,3584]{2,1,0:T(4,128)(2,1)}, u32[]{:S(2)}) copy-start(bf16[1,4,3584]{2,1,0:T(4,128)(2,1)} %param.20) | copy-start | bytes 86020
  190.7 27.1 %all-to-all-start.1 = ((bf16[4,1,256,896]{3,2,1,0:T(8,128)(2,1)}), bf16[4,1,256,896]{3,2,1,0:T(8,128)(2,1)S(1)}, u32[]{:S(2)}, u32[]{:S(2)}) async-start(bf16[4,1,256,896]{3,2,1,0:T(8,128)(2,1)} %bitcast.98), calls=%async_computation.1 | async-start | bytes 3670016 | tf_op jit(solution)/shard_map/all_to_all | solution.py:46
  194.7 23.3 %copy-start.5 = (bf16[256,896]{1,0:T(8,128)(2,1)S(1)}, bf16[256,896]{1,0:T(8,128)(2,1)}, u32[]{:S(2)}) copy-start(bf16[256,896]{1,0:T(8,128)(2,1)} %param.12) | copy-start | bytes 1376260
  227.9 64.2 %all-to-all-start.3 = ((f32[64,1,1]{2,1,0:T(1,128)}), f32[64,1,1]{2,1,0:T(1,128)S(1)}, u32[]{:S(2)}, u32[]{:S(2)}) async-start(f32[64,1,1]{2,1,0:T(1,128)} %broadcast_in_dim.35), calls=%async_computation.3 | async-start | bytes 65536 | tf_op jit(solution)/shard_map/all_to_all | solution.py:52
  292.2 52.6 %all-to-all-start.5 = ((bf16[1,4,3584]{1,0,2:T(2,128)(2,1)}), bf16[1,4,3584]{1,0,2:T(2,128)(2,1)S(1)}, u32[]{:S(2)}, u32[]{:S(2)}) async-start(bf16[1,4,3584]{1,0,2:T(2,128)(2,1)} %copy.129), calls=%async_computation.5 | async-start | bytes 3670016 | tf_op jit(solution)/shard_map/all_to_all | solution.py:167
  299.4 2.1 copy-start.10
  344.8 51.5 %all-to-all-start = ((bf16[1,3584,4]{2,0,1:T(2,128)(2,1)}), bf16[1,3584,4]{2,0,1:T(2,128)(2,1)}, u32[]{:S(2)}, u32[]{:S(2)}) async-start(bf16[1,3584,4]{2,0,1:T(2,128)(2,1)} %copy.112), calls=%async_computation | async-start | bytes 3670016 | tf_op jit(solution)/shard_map/all_to_all | solution.py:166
  396.9 15.3 %all-to-all-start.4 = ((f32[64,1,1]{2,1,0:T(1,128)}), f32[64,1,1]{2,1,0:T(1,128)S(1)}, u32[]{:S(2)}, u32[]{:S(2)}) async-start(f32[64,1,1]{2,1,0:T(1,128)} %broadcast_in_dim.36), calls=%async_computation.4 | async-start | bytes 65536 | tf_op jit(solution)/shard_map/all_to_all | solution.py:52
  407.9 4.9 %copy-start.3 = (f32[64,3584]{0,1:T(8,128)S(1)}, f32[64,3584]{0,1:T(8,128)}, u32[]{:S(2)}) copy-start(f32[64,3584]{0,1:T(8,128)} %copy.127) | copy-start | bytes 2752516
  414.3 6.7 %copy-start.1 = (bf16[256,3584]{1,0:T(8,128)(2,1)S(1)}, bf16[256,3584]{1,0:T(8,128)(2,1)}, u32[]{:S(2)}) copy-start(bf16[256,3584]{1,0:T(8,128)(2,1)} %param.11) | copy-start | bytes 5505028
Sparse Core Ops, SparseCore 0:
  20.4 49.4 all-gather.5
  71.7 21.7 all-gather.7
  96.2 81.5 all-gather.9
where the time goes:
time: 430 us; the launch traced here: 429 us
  waiting for transfers between devices  241 us (56%)
  blocking collectives  71.3 us (17%)
  local copies, waits for them, and re-layouts  38.2 us (9%)
  starting transfers between devices  31.5 us (7%)
  matrix products  18.6 us (4%)
  between operations  17.9 us (4%)
  other arithmetic  10.5 us (2%)
    all_gather x2, waiting for transfers between devices, all_blocks(): parts = lax.all_gather(parts, axes[k], axis=0, tiled=True)  69.5 us
    all_gather x1, waiting for transfers between devices, per_device(): lax.all_gather(w_out, POP, axis=1, tiled=True)  65.1 us
    all_gather x1, blocking collectives, side_by_side(): result, at, done = (lax.all_gather(both, axis, axis=dim, tiled=True), 0, [])  51.8 us
    all_to_all x1, waiting for transfers between devices, per_device(): lax.all_to_all(query_left_factors, POP, split_axis=1, concat_axis=0, tile...  44 us
    all_to_all x1, waiting for transfers between devices, per_device(): lax.all_to_all(o_right, POP, split_axis=2, concat_axis=0, tiled=True)  38.7 us
    all_to_all x1, waiting for transfers between devices, summed_on_arrival(): lax.all_to_all(cut_along(shard, dim, devices), axis, 0, 0, tiled=True)  22.5 us
    all_to_all x2, starting transfers between devices, copy_for_each(): return lax.all_to_all(copies, axis, split_axis=0, concat_axis=0, tiled=True)  14 us
    all_gather x1, blocking collectives, all_blocks(): parts = lax.all_gather(parts, axes[k], axis=0, tiled=True)  13 us
  transfers between devices with their start and end apart: 8, of which 7 were waited for; matrix products, arithmetic and copies ran while one was open for 9% of the time, Pallas kernels for 0%

commit v1 on v0

--- a/solution.py
+++ b/solution.py
@@ -164,7 +164,9 @@
     every_weight = gathered_copies(weight, POP, 0)
     right_factors_gathered, left_all = side_by_side((query_right_factors, o_left), POP, 0, 1)
     rows_q = lax.all_to_all(query_left_factors, POP, split_axis=1, concat_axis=0, tiled=True)
-    cols_o = lax.all_to_all(o_right, POP, split_axis=2, concat_axis=0, tiled=True)
+    cols_o = jnp.concatenate(
+        lax.all_to_all(jnp.stack(jnp.split(o_right, lax.axis_size(POP), axis=2)), POP, 0, 0), axis=0
+    )
     whole_population = rows_q.shape[0]
     left_q = jnp.transpose(
         rows_q.astype(jnp.float32) * every_weight[:, None, None], (1, 0, 2)

time: 430 us -> 355 us (0.83)
  waiting for transfers between devices: 241 us -> 123 us
  local copies, waits for them, and re-layouts: 38.2 us -> 75.5 us
    all_gather x1, waiting for transfers between devices: 65.1 us -> 0.01 us  [per_device(): lax.all_gather(w_out, POP, axis=1, tiled=True)]
    all_to_all x1, waiting for transfers between devices: 38.7 us -> 1.74 us  [per_device(): lax.all_to_all(jnp.stack(jnp.split(o_right, lax.axis_size(POP), axis=2)),...]
    unnamed x35 -> x97, local copies, waits for them, and re-layouts: 12 us -> 48.5 us
    all_gather x2, waiting for transfers between devices: 69.5 us -> 49.6 us  [all_blocks(): parts = lax.all_gather(parts, axes[k], axis=0, tiled=True)]
    all_to_all x2, waiting for transfers between devices: 0.2 us -> 7.13 us  [copy_for_each(): return lax.all_to_all(copies, axis, split_axis=0, concat_axis=0, tiled=True)]
  transfers between devices with their start and end apart: 8 -> 8, of which waited for: 7 -> 6; matrix products, arithmetic and copies ran while one was open for 9% -> 24% of each run, Pallas kernels for 0% -> 0%
where the time goes in v1:
time: 355 us; the launch traced here: 353 us
  waiting for transfers between devices  123 us (35%)
  local copies, waits for them, and re-layouts  75.5 us (21%)
  blocking collectives  70.9 us (20%)
  starting transfers between devices  34 us (10%)
  matrix products  18.8 us (5%)
  between operations  17.8 us (5%)
  other arithmetic  13.4 us (4%)
    all_gather x1, blocking collectives, side_by_side(): result, at, done = (lax.all_gather(both, axis, axis=dim, tiled=True), 0, [])  51.4 us
    all_gather x2, waiting for transfers between devices, all_blocks(): parts = lax.all_gather(parts, axes[k], axis=0, tiled=True)  49.6 us
    unnamed x97, local copies, waits for them, and re-layouts  48.5 us
    all_to_all x1, waiting for transfers between devices, per_device(): lax.all_to_all(query_left_factors, POP, split_axis=1, concat_axis=0, tile...  42.7 us
    all_to_all x1, waiting for transfers between devices, summed_on_arrival(): lax.all_to_all(cut_along(shard, dim, devices), axis, 0, 0, tiled=True)  21.1 us
    all_to_all x2, starting transfers between devices, copy_for_each(): return lax.all_to_all(copies, axis, split_axis=0, concat_axis=0, tiled=True)  15.2 us
    all_gather x1, blocking collectives, all_blocks(): parts = lax.all_gather(parts, axes[k], axis=0, tiled=True)  13 us
    all_to_all x1, starting transfers between devices, per_device(): lax.all_to_all(jnp.stack(jnp.split(o_right, lax.axis_size(POP), axis=2)),...  8.61 us
  transfers between devices with their start and end apart: 8, of which 6 were waited for; matrix products, arithmetic and copies ran while one was open for 24% of the time, Pallas kernels for 0%

profile of v1, /device:TPU:1, one launch (start us, length us, event | category | flops | bytes accessed | tf_op | source)
XLA Modules:
  0.0 353.4 jit_solution(6779498463947155787)
XLA Ops:
  7.2 13.0 %all-gather = bf16[224,896]{1,0:T(8,128)(2,1)} all-gather(bf16[56,896]{1,0:T(8,128)(2,1)} %param.13), channel_id=2, replica_groups=mesh['pop_0'=4,'pop_1'=8,'pop_2'=2,'mp'=4] {'pop_0'}, dimensions={0}, use_global_device_ids=true | all-gather | bytes 501760 | tf_op jit(solution)/shard_map/all_gather | solution.py:28
  20.3 49.6 %all-gather.6.cloned.1.call-done = bf16[32,56,896]{2,1,0:T(8,128)(2,1)} async-done(((bf16[4,56,896]{2,1,0:T(8,128)(2,1)}), bf16[32,56,896]{2,1,0:T(8,128)(2,1)}) %all-gather.6.cloned.1.call-update) | async-done | bytes 3211280 | tf_op jit(solution)/shard_map/all_gather | solution.py:28
  72.6 51.4 %all-gather.1 = bf16[64,1,7168]{2,1,0:T(2,128)(2,1)S(1)} all-gather(bf16[1,1,7168]{2,1,0:T(2,128)(2,1)S(1)} %maximum_bitcast_fusion.2), channel_id=1, replica_groups=mesh['pop_0'=4,'pop_1'=8,'pop_2'=2,'mp'=4] {'pop_0','pop_1','pop_2'}, dimensions={0}, use_global_device_ids=true | all-gather | bytes 931840 | tf_op jit(solution)/shard_map/all_gather | solution.py:66
  165.2 3.4 copy.100
  168.7 2.1 fusion.29
  170.8 2.1 fusion.3
  181.8 2.6 convolution_convert_fusion
  184.5 5.2 %fusion.30 = f32[256,3584]{1,0:T(8,128)S(1)} fusion(bf16[256,896]{0,1:T(8,128)(2,1)S(1)} %bitcast.234, bf16[896,3584]{0,1:T(8,128)(2,1)} %all-gather.10.cloned.1.call-done), kind=kOutput, calls=%fused_computation.122 | convolution fusion | flops 1644167168 | bytes 10551296 | tf_op jit(solution)/shard_map/mtf,fe->mte/dot_general | solution.py:146
  189.7 3.1 fusion.1
  192.8 4.2 %reshape.289 = bf16[1,256,4,896]{3,2,1,0:T(4,128)(2,1)} reshape(bf16[256,3584]{1,0:T(8,128)(2,1)} %fusion.1) | data formatting | bytes 3670016 | tf_op jit(solution)/shard_map/reshape | solution.py:41
  197.1 3.0 copy.128
  200.0 4.5 %all-to-all-start.1 = ((bf16[4,1,256,896]{3,2,1,0:T(8,128)(2,1)}), bf16[4,1,256,896]{3,2,1,0:T(8,128)(2,1)}, u32[]{:S(2)}, u32[]{:S(2)}) async-start(bf16[4,1,256,896]{3,2,1,0:T(8,128)(2,1)} %bitcast.227), calls=%async_computation.1 | async-start | bytes 3670016 | tf_op jit(solution)/shard_map/all_to_all | solution.py:46
  207.0 21.1 %all-to-all-done.1 = bf16[4,1,256,896]{3,2,1,0:T(8,128)(2,1)} async-done(((bf16[4,1,256,896]{3,2,1,0:T(8,128)(2,1)}), bf16[4,1,256,896]{3,2,1,0:T(8,128)(2,1)}, u32[]{:S(2)}, u32[]{:S(2)}) %all-to-all-start.1) | async-done | bytes 1835040 | tf_op jit(solution)/shard_map/all_to_all | solution.py:46
  231.5 6.5 %all_to_all.37 = f32[4,1,1]{2,1,0:T(1,128)S(1)} all-to-all(f32[4,1,1]{2,1,0:T(1,128)S(1)} %broadcast_in_dim.34), channel_id=1, replica_groups=mesh['pop_0'=4,'pop_1'=8,'pop_2'=2,'mp'=4] {'mp'}, dimensions={0} | all-to-all | bytes 32 | tf_op jit(solution)/shard_map/all_to_all | solution.py:52
  239.9 9.1 %all-to-all-start.3 = ((f32[64,1,1]{2,1,0:T(1,128)}), f32[64,1,1]{2,1,0:T(1,128)S(1)}, u32[]{:S(2)}, u32[]{:S(2)}) async-start(f32[64,1,1]{2,1,0:T(1,128)} %broadcast_in_dim.35), calls=%async_computation.3 | async-start | bytes 65536 | tf_op jit(solution)/shard_map/all_to_all | solution.py:52
  249.7 3.2 copy.98
  252.9 5.4 %all-to-all-done.3 = f32[64,1,1]{2,1,0:T(1,128)S(1)} async-done(((f32[64,1,1]{2,1,0:T(1,128)}), f32[64,1,1]{2,1,0:T(1,128)S(1)}, u32[]{:S(2)}, u32[]{:S(2)}) %all-to-all-start.3) | async-done | bytes 288 | tf_op jit(solution)/shard_map/all_to_all | solution.py:52
  258.3 5.6 %all-to-all-start = ((bf16[1,3584,4]{2,0,1:T(2,128)(2,1)}), bf16[1,3584,4]{2,0,1:T(2,128)(2,1)}, u32[]{:S(2)}, u32[]{:S(2)}) async-start(bf16[1,3584,4]{2,0,1:T(2,128)(2,1)} %copy.98), calls=%async_computation | async-start | bytes 3670016 | tf_op jit(solution)/shard_map/all_to_all | solution.py:166
  266.6 42.7 %all-to-all-done = bf16[1,3584,4]{2,0,1:T(2,128)(2,1)} async-done(((bf16[1,3584,4]{2,0,1:T(2,128)(2,1)}), bf16[1,3584,4]{2,0,1:T(2,128)(2,1)}, u32[]{:S(2)}, u32[]{:S(2)}) %all-to-all-start) | async-done | bytes 28704 | tf_op jit(solution)/shard_map/all_to_all | solution.py:166
  309.9 6.0 %all-to-all-start.4 = ((f32[64,1,1]{2,1,0:T(1,128)}), f32[64,1,1]{2,1,0:T(1,128)S(1)}, u32[]{:S(2)}, u32[]{:S(2)}) async-start(f32[64,1,1]{2,1,0:T(1,128)} %broadcast_in_dim.36), calls=%async_computation.4 | async-start | bytes 65536 | tf_op jit(solution)/shard_map/all_to_all | solution.py:52
  319.6 3.6 %copy.99 = bf16[1,3584,4]{1,2,0:T(4,128)(2,1)S(1)} copy(bf16[1,3584,4]{2,0,1:T(2,128)(2,1)} %all-to-all-done) | data formatting | bytes 57344 | tf_op jit(solution)/shard_map/all_to_all | solution.py:166
  325.1 8.6 %all-to-all-start.5 = ((bf16[64,1,4,56]{3,2,1,0:T(4,128)(2,1)}), bf16[64,1,4,56]{3,2,1,0:T(4,128)(2,1)S(1)}, u32[]{:S(2)}, u32[]{:S(2)}) async-start(bf16[64,1,4,56]{3,2,1,0:T(4,128)(2,1)} %constant_dynamic-update-slice_fusion), calls=%async_computation.5 | async-start | bytes 131072 | tf_op jit(solution)/shard_map/all_to_all | solution.py:168
  334.3 3.1 multiply_bitcast_fusion
  337.5 2.7 copy.114
  (139 shorter events, 73.7 us)
Async XLA Ops:
  7.2 155.8 %copy-start = (bf16[256,3584]{1,0:T(8,128)(2,1)S(1)}, bf16[256,3584]{1,0:T(8,128)(2,1)}, u32[]{:S(2)}) copy-start(bf16[256,3584]{1,0:T(8,128)(2,1)} %param.11) | copy-start | bytes 5505028
  7.2 62.7 %all-gather.6.cloned.1.call-start = ((), (), s32[]{:S(2)}) async-start(), calls=%async_computation.6 | async-start | bytes 3612672 | tf_op jit(solution)/shard_map/all_gather | solution.py:28
  20.2 51.8 %copy-start.12 = (bf16[1,896,4]{1,2,0:T(4,128)(2,1)S(1)}, bf16[1,896,4]{1,2,0:T(4,128)(2,1)}, u32[]{:S(2)}) copy-start(bf16[1,896,4]{1,2,0:T(4,128)(2,1)} %param.19) | copy-start | bytes 21508
  20.3 145.0 %all-gather.8.cloned.1.call-start = ((), (), s32[]{:S(2)}) async-start(), calls=%async_computation.7 | async-start | bytes 9633792 | tf_op jit(solution)/shard_map/all_gather | solution.py:28
  69.9 2.6 copy-start.11
  69.9 114.6 %all-gather.10.cloned.1.call-start = ((), (), s32[]{:S(2)}) async-start(), calls=%async_computation.8 | async-start | bytes 6522880 | tf_op jit(solution)/shard_map/all_gather | solution.py:149
  124.0 1.2 copy-start.6
  124.0 39.0 %copy-start.4 = (bf16[3584,128]{1,0:T(8,128)(2,1)S(1)}, bf16[3584,128]{1,0:T(8,128)(2,1)}, u32[]{:S(2)}) copy-start(bf16[3584,128]{1,0:T(8,128)(2,1)} %param.14) | copy-start | bytes 2752516
  168.7 2.1 copy-start.9
  177.9 1.5 copy-start.7
  177.9 1.5 copy-start.8
  180.0 1.3 copy-start.1
  180.0 1.8 copy-start.13
  200.0 5.8 %copy-start.2 = (bf16[64,1,7168]{2,0,1:T(8,128)(2,1)S(1)}, bf16[64,1,7168]{2,0,1:T(8,128)(2,1)}, u32[]{:S(2)}) copy-start(bf16[64,1,7168]{2,0,1:T(8,128)(2,1)} %copy.129) | copy-start | bytes 2752516
  200.0 28.1 %all-to-all-start.1 = ((bf16[4,1,256,896]{3,2,1,0:T(8,128)(2,1)}), bf16[4,1,256,896]{3,2,1,0:T(8,128)(2,1)}, u32[]{:S(2)}, u32[]{:S(2)}) async-start(bf16[4,1,256,896]{3,2,1,0:T(8,128)(2,1)} %bitcast.227), calls=%async_computation.1 | async-start | bytes 3670016 | tf_op jit(solution)/shard_map/all_to_all | solution.py:46
  207.0 23.0 %copy-start.5 = (bf16[256,896]{1,0:T(8,128)(2,1)S(1)}, bf16[256,896]{1,0:T(8,128)(2,1)}, u32[]{:S(2)}) copy-start(bf16[256,896]{1,0:T(8,128)(2,1)} %param.12) | copy-start | bytes 1376260
  207.0 42.6 %copy-start.10 = (bf16[1,3584,4]{1,2,0:T(4,128)(2,1)S(1)}, bf16[1,3584,4]{1,2,0:T(4,128)(2,1)}, u32[]{:S(2)}) copy-start(bf16[1,3584,4]{1,2,0:T(4,128)(2,1)} %param.17) | copy-start | bytes 86020
  239.9 18.4 %all-to-all-start.3 = ((f32[64,1,1]{2,1,0:T(1,128)}), f32[64,1,1]{2,1,0:T(1,128)S(1)}, u32[]{:S(2)}, u32[]{:S(2)}) async-start(f32[64,1,1]{2,1,0:T(1,128)} %broadcast_in_dim.35), calls=%async_computation.3 | async-start | bytes 65536 | tf_op jit(solution)/shard_map/all_to_all | solution.py:52
  252.9 63.7 %copy-start.3 = (f32[64,3584]{1,0:T(8,128)S(1)}, f32[64,3584]{1,0:T(8,128)}, u32[]{:S(2)}) copy-start(f32[64,3584]{1,0:T(8,128)} %get-tuple-element.5) | copy-start | bytes 2752516
  258.3 51.0 %all-to-all-start = ((bf16[1,3584,4]{2,0,1:T(2,128)(2,1)}), bf16[1,3584,4]{2,0,1:T(2,128)(2,1)}, u32[]{:S(2)}, u32[]{:S(2)}) async-start(bf16[1,3584,4]{2,0,1:T(2,128)(2,1)} %copy.98), calls=%async_computation | async-start | bytes 3670016 | tf_op jit(solution)/shard_map/all_to_all | solution.py:166
  309.9 15.3 %all-to-all-start.4 = ((f32[64,1,1]{2,1,0:T(1,128)}), f32[64,1,1]{2,1,0:T(1,128)S(1)}, u32[]{:S(2)}, u32[]{:S(2)}) async-start(f32[64,1,1]{2,1,0:T(1,128)} %broadcast_in_dim.36), calls=%async_computation.4 | async-start | bytes 65536 | tf_op jit(solution)/shard_map/all_to_all | solution.py:52
  325.1 18.4 %all-to-all-start.5 = ((bf16[64,1,4,56]{3,2,1,0:T(4,128)(2,1)}), bf16[64,1,4,56]{3,2,1,0:T(4,128)(2,1)S(1)}, u32[]{:S(2)}, u32[]{:S(2)}) async-start(bf16[64,1,4,56]{3,2,1,0:T(4,128)(2,1)} %constant_dynamic-update-slice_fusion), calls=%async_computation.5 | async-start | bytes 131072 | tf_op jit(solution)/shard_map/all_to_all | solution.py:168
Sparse Core Ops, SparseCore 0:
  20.4 49.4 all-gather.5
  71.7 21.7 all-gather.7
  96.2 81.9 all-gather.9
